TPU v7x, 32 devices: a whole 2x2x4 slice. The times are simulated.
32 devices in a mesh: dp: 2 (over x), expert: 8 (over z, core), tensor: 2 (over y).
Axes of the slice: x: 2, y: 2, z: 4, core: 2. Of those that a mesh axis runs over, the one named last changes fastest.
Arguments:
- tokens: bfloat16 [192, 256, 1280], P(('dp', 'expert', 'tensor')), may hold values from -16 to 16
- cotangent: bfloat16 [192, 256, 1280], P(('dp', 'expert', 'tensor')), may hold values from -6 to 6
- norm_gain: float32 [1280], replicated, may hold values from 0.5 to 1.5
- slot_keys: bfloat16 [1280, 16], replicated, may hold values from -2 to 2
- w_in: bfloat16 [8, 1280, 2560], P('expert', None, 'tensor'), may hold values from -0.15625 to 0.15625
- w_out: bfloat16 [8, 2560, 1280], P('expert', 'tensor'), may hold values from -0.125 to 0.125
Outputs:
- grad_tokens: bfloat16 [192, 256, 1280], P(('dp', 'expert', 'tensor'))
- grad_gain: float32 [1280], replicated
- grad_keys: float32 [1280, 16], replicated
- grad_in: bfloat16 [8, 1280, 2560], P('expert', 'dp', 'tensor')
- grad_out: bfloat16 [8, 2560, 1280], P('expert', 'tensor', 'dp')
All inputs are finite; a program needn't handle non-finite values.
Results may differ from a plain program's by a relative error of at most 0.014.
The roundings to bfloat16 on the way count: a program that leaves them out, or rounds other values in their place, can miss the bound.
Values may be sent and summed in bfloat16 or wider, within the bound.
A program may use at most 128 MiB of HBM per device.

v0:
```python
import jax
import jax.numpy as jnp
from jax import lax
from jax.sharding import PartitionSpec as P

SLOT_PER = 2


EPSILON = 1e-06


def mixing_forward(tokens, gain, slot_keys):
    average = jnp.mean(tokens, axis=-1, keepdims=True, dtype=jnp.float32)
    centred = tokens.astype(jnp.float32) - average
    spread = jnp.mean(centred * centred, axis=-1, keepdims=True)
    inverse = lax.rsqrt(spread + EPSILON)
    scaled = centred * inverse
    normed = (scaled * gain).astype(jnp.bfloat16)
    logits = jnp.einsum("bmd,dn->bmn", normed, slot_keys, preferred_element_type=jnp.float32)
    dispatch = jax.nn.softmax(logits, axis=1)
    combine = jax.nn.softmax(logits, axis=2)
    dispatch_low = dispatch.astype(jnp.bfloat16)
    slot_values = jnp.einsum(
        "bmn,bmd->bnd", dispatch_low, normed, preferred_element_type=jnp.float32
    )
    return (slot_values, combine, (scaled, inverse, normed, dispatch, combine, dispatch_low))


def mixing_backward(saved, gain, slot_keys, slot_grad, combine_grad):
    scaled, inverse, normed, dispatch, combine, dispatch_low = saved
    grad_dispatch = jnp.einsum(
        "bnd,bmd->bmn", slot_grad, normed, preferred_element_type=jnp.float32
    )
    grad_normed = jnp.einsum(
        "bmn,bnd->bmd", dispatch_low, slot_grad, preferred_element_type=jnp.float32
    )
    grad_logits = dispatch * (
        grad_dispatch - jnp.sum(dispatch * grad_dispatch, axis=1, keepdims=True)
    )
    grad_logits = grad_logits + combine * (
        combine_grad - jnp.sum(combine * combine_grad, axis=2, keepdims=True)
    )
    keys_wide = slot_keys.astype(jnp.float32)
    grad_normed = grad_normed + jnp.einsum(
        "bmn,dn->bmd", grad_logits, keys_wide, precision=lax.Precision.HIGHEST
    )
    keys_term = jnp.einsum(
        "bmd,bmn->dn", normed.astype(jnp.float32), grad_logits, precision=lax.Precision.HIGHEST
    )
    gain_term = jnp.sum(grad_normed * scaled, axis=(0, 1))
    grad_scaled = grad_normed * gain
    first_mean = jnp.mean(grad_scaled, axis=-1, keepdims=True)
    second_mean = jnp.mean(grad_scaled * scaled, axis=-1, keepdims=True)
    grad_tok = inverse * (grad_scaled - first_mean - scaled * second_mean)
    return (grad_tok, gain_term, keys_term)


def contract_rows(left, right):
    return lax.dot_general(
        left, right, (((0,), (0,)), ((), ())), preferred_element_type=jnp.float32
    )


def contract_cols(left, right):
    return lax.dot_general(
        left, right, (((1,), (1,)), ((), ())), preferred_element_type=jnp.float32
    )


def local(tokens, cotangent, norm_gain, slot_keys, w_in, w_out):
    local_imgs, token_count, features = tokens.shape
    slot_count = slot_keys.shape[1]
    experts = slot_count // SLOT_PER
    slot_values, combine, saved = mixing_forward(tokens, norm_gain, slot_keys)
    slot_inputs = slot_values.astype(jnp.bfloat16).reshape(local_imgs, experts, SLOT_PER, features)
    arrived = lax.all_to_all(slot_inputs, "expert", split_axis=1, concat_axis=0, tiled=True)
    slot_rows = lax.all_gather(arrived, "tensor", axis=0, tiled=True).reshape(-1, features)
    first_proj = w_in[0]
    second_proj = w_out[0]
    pre_act = jnp.dot(slot_rows, first_proj, preferred_element_type=jnp.float32)
    hidden = jax.nn.gelu(pre_act).astype(jnp.bfloat16)
    segment = hidden
    outputs = lax.psum_scatter(
        jnp.dot(segment, second_proj, preferred_element_type=jnp.float32),
        "tensor",
        scatter_dimension=0,
        tiled=True,
    )
    outputs = outputs.astype(jnp.bfloat16).reshape(arrived.shape)
    returned = lax.all_to_all(outputs, "expert", split_axis=0, concat_axis=1, tiled=True).reshape(
        local_imgs, slot_count, features
    )
    combine_low = combine.astype(jnp.bfloat16)
    grad_slots = jnp.einsum(
        "bmn,bmd->bnd", combine_low, cotangent, preferred_element_type=jnp.float32
    )
    grad_slots = grad_slots.astype(jnp.bfloat16).reshape(local_imgs, experts, SLOT_PER, features)
    grad_combine = jnp.einsum(
        "bmd,bnd->bmn", cotangent, returned, preferred_element_type=jnp.float32
    )
    grads_sent = lax.all_to_all(grad_slots, "expert", split_axis=1, concat_axis=0, tiled=True)
    grad_rows = lax.all_gather(grads_sent, "tensor", axis=0, tiled=True).reshape(-1, features)
    grad_hidden = contract_cols(grad_rows, second_proj)
    grad_pre = jax.vjp(jax.nn.gelu, pre_act)[1](grad_hidden)[0].astype(jnp.bfloat16)
    segment = grad_pre
    grad_in_rows = lax.psum_scatter(
        contract_cols(segment, first_proj), "tensor", scatter_dimension=0, tiled=True
    )
    grad_in_rows = grad_in_rows.astype(jnp.bfloat16).reshape(arrived.shape)
    grad_back = lax.all_to_all(
        grad_in_rows, "expert", split_axis=0, concat_axis=1, tiled=True
    ).reshape(local_imgs, slot_count, features)
    grad_tok, gain_term, keys_term = mixing_backward(
        saved, norm_gain, slot_keys, grad_back, grad_combine
    )
    grad_tokens = (cotangent.astype(jnp.float32) + grad_tok).astype(jnp.bfloat16)
    grad_gain, grad_keys = lax.psum((gain_term, keys_term), ("dp", "expert", "tensor"))
    split_rows, split_grads = (
        lax.all_to_all(slot_rows, "dp", split_axis=1, concat_axis=0, tiled=True),
        lax.all_to_all(grad_rows, "dp", split_axis=1, concat_axis=0, tiled=True),
    )
    first_total = contract_rows(split_rows, lax.all_gather(grad_pre, "dp", axis=0, tiled=True))
    second_total = contract_rows(lax.all_gather(hidden, "dp", axis=0, tiled=True), split_grads)
    return (
        grad_tokens,
        grad_gain,
        grad_keys,
        first_total.astype(jnp.bfloat16)[None],
        second_total.astype(jnp.bfloat16)[None],
    )


def solution(mesh):
    placed = (
        P(("dp", "expert", "tensor"), None, None),
        P(("dp", "expert", "tensor"), None, None),
        P(),
        P(),
        P("expert", None, "tensor"),
        P("expert", "tensor", None),
    )
    return jax.shard_map(
        local,
        mesh=mesh,
        in_specs=placed,
        out_specs=(
            P(("dp", "expert", "tensor"), None, None),
            P(),
            P(),
            P("expert", "dp", "tensor"),
            P("expert", "tensor", "dp"),
        ),
        check_vma=False,
    )
```

profile of v0, /device:TPU:0, one launch (start us, length us, event | category | flops | bytes accessed | tf_op | source)
XLA Modules:
  0.0 314.0 jit_solution(6597556359371723776)
XLA Ops:
  7.2 2.8 convert_reduce_fusion
  10.1 3.4 %fusion.15 = f32[6,256]{1,0:T(8,128)S(1)} fusion(bf16[6,256,1280]{2,1,0:T(8,128)(2,1)} %param.6, f32[6,256]{1,0:T(8,128)S(1)} %broadcast_multiply_fusion.2), kind=kLoop, calls=%fused_computation.17 | loop fusion | flops 7862784 | bytes 3944448 | tf_op jit(solution)/shard_map/reduce_sum | solution.py:15
  15.9 4.2 %convolution_convert_fusion.2 = bf16[6,16,1280]{2,1,0:T(8,128)(2,1)} fusion(f32[6,16]{1,0:T(8,128)S(1)} %get-tuple-element.8, f32[6,256,16]{1,2,0:T(8,128)S(1)} %fusion.41, bf16[6,256,1280]{2,1,0:T(8,128)(2,1)} %param.6, f32[1280]{0:T(1024)S(1)} %copy-done.6, f32[6,256]{1,0:T(8,128)S(1)} %add_rsqrt_fusion, f32[6,256]{1,0:T(8,128)S(1)} %broadcast_multiply_fusion.2), kind=kOutput, calls=%fused_computation.32 | convolution fusion | flops 72941920 | bytes 4294016 | tf_op jit(solution)/shard_map/bmn,bmd->bnd/dot_general | solution.py:23
  22.0 6.4 %all-to-all-start.1 = ((bf16[6,8,2,1280]{3,2,0,1:T(2,128)(2,1)}), bf16[6,8,2,1280]{3,2,0,1:T(2,128)(2,1)S(1)}, u32[]{:S(2)}, u32[]{:S(2)}) async-start(bf16[6,8,2,1280]{3,2,0,1:T(2,128)(2,1)} %copy.39), calls=%async_computation.1 | async-start | bytes 491520 | tf_op jit(solution)/shard_map/all_to_all | solution.py:76
  30.0 3.5 %convolution_convert_fusion.3 = bf16[6,16,1280]{2,1,0:T(8,128)(2,1)} fusion(bf16[6,256,1280]{2,1,0:T(8,128)(2,1)} %param.7, f32[6,256]{1,0:T(8,128)S(1)} %get-tuple-element.10, f32[6,256,16]{1,2,0:T(8,128)} %copy-done.3), kind=kOutput, calls=%fused_computation.33 | convolution fusion | flops 63112720 | bytes 4282368 | tf_op jit(solution)/shard_map/bmn,bmd->bnd/dot_general | solution.py:94
  37.7 4.5 %all-to-all-start = ((bf16[6,8,2,1280]{3,2,0,1:T(2,128)(2,1)}), bf16[6,8,2,1280]{3,2,0,1:T(2,128)(2,1)}, u32[]{:S(2)}, u32[]{:S(2)}) async-start(bf16[6,8,2,1280]{3,2,0,1:T(2,128)(2,1)} %copy.37), calls=%async_computation | async-start | bytes 491520 | tf_op jit(solution)/shard_map/all_to_all | solution.py:101
  42.2 9.1 %all_gather.13 = bf16[96,1,2,1280]{3,2,1,0:T(2,128)(2,1)} all-gather(bf16[48,1,2,1280]{3,2,1,0:T(2,128)(2,1)S(1)} %bitcast.84), channel_id=1, replica_groups=mesh['dp'=2,'expert'=8,'tensor'=2] {'tensor'}, dimensions={0}, use_global_device_ids=true | all-gather | bytes 737280 | tf_op jit(solution)/shard_map/all_gather | solution.py:77
  51.3 2.0 reshape.74
  53.3 11.1 %all_gather.12 = bf16[96,1,2,1280]{3,2,1,0:T(2,128)(2,1)} all-gather(bf16[48,1,2,1280]{3,2,1,0:T(2,128)(2,1)} %bitcast.4), channel_id=1, replica_groups=mesh['dp'=2,'expert'=8,'tensor'=2] {'tensor'}, dimensions={0}, use_global_device_ids=true | all-gather | bytes 737280 | tf_op jit(solution)/shard_map/all_gather | solution.py:102
  64.3 2.0 reshape.72
  66.3 2.7 multiply_convert_fusion
  69.0 3.5 %fusion.36 = bf16[192,1280]{1,0:T(8,128)(2,1)S(1)} fusion(f32[192,1280]{1,0:T(8,128)S(1)} %get-tuple-element.13, bf16[192,1280]{1,0:T(8,128)(2,1)} %reshape.72, bf16[1,1280,1280]{2,1,0:T(8,128)(2,1)} %param.11), kind=kOutput, calls=%fused_computation.48 | convolution fusion | flops 634060800 | bytes 5242880 | tf_op jit(solution)/shard_map/dot_general | solution.py:65
  73.3 2.2 fusion.16
  75.6 3.8 %fusion.20 = f32[192,1280]{1,0:T(8,128)} fusion(bf16[192,1280]{1,0:T(8,128)(2,1)} %get-tuple-element.12, bf16[1,1280,1280]{2,1,0:T(8,128)(2,1)} %param.11), kind=kOutput, calls=%fused_computation.24 | convolution fusion | flops 629145600 | bytes 4751360 | tf_op jit(solution)/shard_map/dot_general | solution.py:84
  79.4 2.1 all_to_all.90
  81.6 2.1 all_to_all.94
  85.6 4.2 %all-to-all-start.4 = ((bf16[192,2,640]{2,0,1:T(8,128)(2,1)}), bf16[192,2,640]{2,0,1:T(8,128)(2,1)}, u32[]{:S(2)}, u32[]{:S(2)}) async-start(bf16[192,2,640]{2,0,1:T(8,128)(2,1)} %copy.45), calls=%async_computation.6 | async-start | bytes 983040 | tf_op jit(solution)/shard_map/all_to_all | solution.py:119
  91.7 15.8 %all_gather.14 = bf16[384,1280]{1,0:T(8,128)(2,1)} all-gather(bf16[192,1280]{1,0:T(8,128)(2,1)} %copy-done.2), channel_id=1, replica_groups=mesh['dp'=2,'expert'=8,'tensor'=2] {'dp'}, dimensions={0}, use_global_device_ids=true | all-gather | bytes 1474560 | tf_op jit(solution)/shard_map/all_gather | solution.py:122
  107.5 4.2 %all-to-all-start.5 = ((bf16[192,2,640]{2,0,1:T(8,128)(2,1)}), bf16[192,2,640]{2,0,1:T(8,128)(2,1)}, u32[]{:S(2)}, u32[]{:S(2)}) async-start(bf16[192,2,640]{2,0,1:T(8,128)(2,1)} %copy.46), calls=%async_computation.7 | async-start | bytes 983040 | tf_op jit(solution)/shard_map/all_to_all | solution.py:120
  111.7 17.8 %all_gather.15 = bf16[384,1280]{1,0:T(8,128)(2,1)} all-gather(bf16[192,1280]{1,0:T(8,128)(2,1)} %get-tuple-element.12), channel_id=1, replica_groups=mesh['dp'=2,'expert'=8,'tensor'=2] {'dp'}, dimensions={0}, use_global_device_ids=true | all-gather | bytes 1474560 | tf_op jit(solution)/shard_map/all_gather | solution.py:123
  131.4 3.6 %all-to-all-start.2 = ((bf16[48,1,2,1280]{3,2,1,0:T(2,128)(2,1)}), bf16[48,1,2,1280]{3,2,1,0:T(2,128)(2,1)S(1)}, u32[]{:S(2)}, u32[]{:S(2)}) async-start(bf16[48,1,2,1280]{3,2,1,0:T(2,128)(2,1)} %bitcast.85), calls=%async_computation.3 | async-start | bytes 491520 | tf_op jit(solution)/shard_map/all_to_all | solution.py:110
  135.0 3.6 %fusion.24 = bf16[1,640,1280]{2,1,0:T(8,128)(2,1)} fusion(bf16[384,640]{1,0:T(8,128)(2,1)} %bitcast.20, bf16[384,1280]{1,0:T(8,128)(2,1)} %all_gather.14), kind=kOutput, calls=%fused_computation.30 | convolution fusion | flops 629964800 | bytes 3112960 | tf_op jit(solution)/shard_map/dot_general | solution.py:59
  138.6 3.6 %fusion.25 = bf16[1,1280,640]{2,1,0:T(8,128)(2,1)} fusion(bf16[384,1280]{1,0:T(8,128)(2,1)} %all_gather.15, bf16[384,640]{1,0:T(8,128)(2,1)} %bitcast.23), kind=kOutput, calls=%fused_computation.31 | convolution fusion | flops 629964800 | bytes 3112960 | tf_op jit(solution)/shard_map/dot_general | solution.py:59
  145.7 5.1 %all-to-all-start.3 = ((bf16[48,1,2,1280]{3,2,1,0:T(2,128)(2,1)}), bf16[48,1,2,1280]{3,2,1,0:T(2,128)(2,1)}, u32[]{:S(2)}, u32[]{:S(2)}) async-start(bf16[48,1,2,1280]{3,2,1,0:T(2,128)(2,1)} %bitcast.86), calls=%async_computation.5 | async-start | bytes 491520 | tf_op jit(solution)/shard_map/all_to_all | solution.py:90
  152.7 4.1 %multiply_reduce_fusion.2 = (f32[6,16]{1,0:T(8,128)S(1)}, f32[6,256,16]{1,2,0:T(8,128)}) fusion(f32[6,256,16]{1,2,0:T(8,128)} %get-tuple-element.9, f32[6,16]{1,0:T(8,128)S(1)} %get-tuple-element.8, bf16[6,16,1280]{2,1,0:T(8,128)(2,1)S(1)} %reshape.76, bf16[6,256,1280]{2,1,0:T(8,128)(2,1)} %param.6, f32[1280]{0:T(1024)} %param.8, ...), kind=kOutput, calls=%fused_computation.54 | convolution fusion | flops 72818592 | bytes 4392704 | tf_op jit(solution)/shard_map/bnd,bmd->bmn/dot_general | solution.py:31
  156.9 5.4 %fusion.43 = f32[6,256,1280]{2,1,0:T(8,128)} fusion(bf16[6,16,1280]{2,1,0:T(8,128)(2,1)S(1)} %reshape.76, f32[6,16]{1,0:T(8,128)S(1)} %get-tuple-element.8, f32[6,256,16]{1,2,0:T(8,128)} %copy-done.3), kind=kOutput, calls=%fused_computation.61 | convolution fusion | flops 62988640 | bytes 8208768 | tf_op jit(solution)/shard_map/bmn,bnd->bmd/dot_general | solution.py:34
  165.1 3.3 %multiply_reduce_fusion.1 = (f32[6,256]{1,0:T(8,128)S(1)}, f32[6,256,16]{1,2,0:T(8,128)S(1)}) fusion(f32[6,256,16]{1,2,0:T(8,128)} %get-tuple-element.11, f32[6,256]{1,0:T(8,128)S(1)} %get-tuple-element.10, bf16[6,16,1280]{2,1,0:T(8,128)(2,1)S(1)} %reshape.78, bf16[6,256,1280]{2,1,0:T(8,128)(2,1)} %param.7), kind=kOutput, calls=%fused_computation.53 | convolution fusion | flops 62986752 | bytes 4386816 | tf_op jit(solution)/shard_map/bmd,bnd->bmn/dot_general | solution.py:98
  169.5 4.5 %convolution_bitcast_fusion = f32[1280,16]{0,1:T(8,128)} fusion(f32[6,256,16]{1,2,0:T(8,128)S(1)} %multiply_add_fusion, bf16[6,256,1280]{2,1,0:T(8,128)(2,1)} %param.6, f32[1280]{0:T(1024)} %param.8, f32[6,256]{1,0:T(8,128)S(1)} %add_rsqrt_fusion, f32[6,256]{1,0:T(8,128)S(1)} %broadcast_multiply_fusion.2), kind=kOutput, calls=%fused_computation.34 | convolution fusion | flops 387317760 | bytes 4129792 | tf_op jit(solution)/shard_map/bmd,bmn->dn/dot_general | solution.py:47
  174.0 10.6 %fusion.14 = (f32[1280]{0:T(1024)S(1)}, f32[6,256]{1,0:T(8,128)S(1)}, f32[6,256]{1,0:T(8,128)S(1)}, f32[6,256,1280]{2,1,0:T(8,128)}) fusion(bf16[6,256,1280]{2,1,0:T(8,128)(2,1)} %param.6, f32[6,256]{1,0:T(8,128)S(1)} %add_rsqrt_fusion, f32[6,256]{1,0:T(8,128)S(1)} %broadcast_multiply_fusion.2, f32[1280]{0:T(1024)S(1)} %copy-done.7, ...), kind=kOutput, calls=%fused_computation.16 | convolution fusion | flops 397143808 | bytes 19834880 | tf_op jit(solution)/shard_map/bmn,dn->bmd/dot_general | solution.py:44
  184.6 8.4 %fusion.13 = bf16[6,256,1280]{2,1,0:T(8,128)(2,1)} fusion(bf16[6,256,1280]{2,1,0:T(8,128)(2,1)} %param.6, bf16[6,256,1280]{2,1,0:T(8,128)(2,1)} %param.7, f32[6,256,1280]{2,1,0:T(8,128)} %get-tuple-element.18, f32[6,256]{1,0:T(8,128)S(1)} %get-tuple-element.19, f32[6,256]{1,0:T(8,128)S(1)} %get-tuple-element.20, f32[1280]{0:T(1024)S(1)} %copy-done.7, ...), kind=kLoop, calls=%fused_computation.15 | loop fusion | flops 21626880 | bytes 19690496 | tf_op jit(solution)/shard_map/convert_element_type | solution.py:116
  193.0 39.8 %psum.14 = f32[1280]{0:T(1024)} all-reduce(f32[1280]{0:T(1024)S(1)} %get-tuple-element.5), channel_id=1, replica_groups=mesh['dp'=2,'expert'=8,'tensor'=2] {'dp','expert','tensor'}, use_global_device_ids=true, to_apply=%region_13.0 | all-reduce | flops 1280 | bytes 10240 | tf_op jit(solution)/shard_map/psum | solution.py:117
  232.8 73.2 %all-reduce.2.cloned.1.call-done = f32[1280,16]{0,1:T(8,128)} async-done(((f32[1280,16]{0,1:T(8,128)}), f32[1280,16]{0,1:T(8,128)}) %all-reduce.2.cloned.1.call-update) | async-done | bytes 81936 | tf_op jit(solution)/shard_map/psum | solution.py:117
  (52 shorter events, 27.6 us)
Async XLA Ops:
  7.2 59.2 %copy-start = (bf16[1,1280,1280]{2,1,0:T(8,128)(2,1)S(1)}, bf16[1,1280,1280]{2,1,0:T(8,128)(2,1)}, u32[]{:S(2)}) copy-start(bf16[1,1280,1280]{2,1,0:T(8,128)(2,1)} %param.10) | copy-start | bytes 9830404
  7.2 6.3 %copy-start.1 = (bf16[6,256,1280]{2,1,0:T(8,128)(2,1)S(1)}, bf16[6,256,1280]{2,1,0:T(8,128)(2,1)}, u32[]{:S(2)}) copy-start(bf16[6,256,1280]{2,1,0:T(8,128)(2,1)} %param.6) | copy-start | bytes 11796484
  7.2 6.3 %copy-start.6 = (f32[1280]{0:T(1024)S(1)}, f32[1280]{0:T(1024)}, u32[]{:S(2)}) copy-start(f32[1280]{0:T(1024)} %param.8) | copy-start | bytes 15364
  7.2 6.3 %copy-start.4 = (bf16[1280,16]{0,1:T(8,128)(2,1)S(1)}, bf16[1280,16]{0,1:T(8,128)(2,1)}, u32[]{:S(2)}) copy-start(bf16[1280,16]{0,1:T(8,128)(2,1)} %param.9) | copy-start | bytes 122884
  15.1 0.8 copy-start.3
  22.0 15.7 %all-to-all-start.1 = ((bf16[6,8,2,1280]{3,2,0,1:T(2,128)(2,1)}), bf16[6,8,2,1280]{3,2,0,1:T(2,128)(2,1)S(1)}, u32[]{:S(2)}, u32[]{:S(2)}) async-start(bf16[6,8,2,1280]{3,2,0,1:T(2,128)(2,1)} %copy.39), calls=%async_computation.1 | async-start | bytes 491520 | tf_op jit(solution)/shard_map/all_to_all | solution.py:76
  37.7 15.6 %all-to-all-start = ((bf16[6,8,2,1280]{3,2,0,1:T(2,128)(2,1)}), bf16[6,8,2,1280]{3,2,0,1:T(2,128)(2,1)}, u32[]{:S(2)}, u32[]{:S(2)}) async-start(bf16[6,8,2,1280]{3,2,0,1:T(2,128)(2,1)} %copy.37), calls=%async_computation | async-start | bytes 491520 | tf_op jit(solution)/shard_map/all_to_all | solution.py:101
  42.2 87.4 %reduce-scatter.3.cloned.1.call-start = ((), (), s32[]{:S(2)}) async-start(), calls=%async_computation.8 | async-start | bytes 1474560 | tf_op jit(solution)/shard_map/reduce_scatter | solution.py:106
  72.5 0.8 copy-start.2
  75.5 66.7 %reduce-scatter.5.cloned.1.call-start = ((), (), s32[]{:S(2)}) async-start(), calls=%async_computation.9 | async-start | bytes 1474560 | tf_op jit(solution)/shard_map/reduce_scatter | solution.py:83
  85.6 22.0 %all-to-all-start.4 = ((bf16[192,2,640]{2,0,1:T(8,128)(2,1)}), bf16[192,2,640]{2,0,1:T(8,128)(2,1)}, u32[]{:S(2)}, u32[]{:S(2)}) async-start(bf16[192,2,640]{2,0,1:T(8,128)(2,1)} %copy.45), calls=%async_computation.6 | async-start | bytes 983040 | tf_op jit(solution)/shard_map/all_to_all | solution.py:119
  107.5 23.9 %all-to-all-start.5 = ((bf16[192,2,640]{2,0,1:T(8,128)(2,1)}), bf16[192,2,640]{2,0,1:T(8,128)(2,1)}, u32[]{:S(2)}, u32[]{:S(2)}) async-start(bf16[192,2,640]{2,0,1:T(8,128)(2,1)} %copy.46), calls=%async_computation.7 | async-start | bytes 983040 | tf_op jit(solution)/shard_map/all_to_all | solution.py:120
  131.4 14.3 %all-to-all-start.2 = ((bf16[48,1,2,1280]{3,2,1,0:T(2,128)(2,1)}), bf16[48,1,2,1280]{3,2,1,0:T(2,128)(2,1)S(1)}, u32[]{:S(2)}, u32[]{:S(2)}) async-start(bf16[48,1,2,1280]{3,2,1,0:T(2,128)(2,1)} %bitcast.85), calls=%async_computation.3 | async-start | bytes 491520 | tf_op jit(solution)/shard_map/all_to_all | solution.py:110
  145.7 16.5 %all-to-all-start.3 = ((bf16[48,1,2,1280]{3,2,1,0:T(2,128)(2,1)}), bf16[48,1,2,1280]{3,2,1,0:T(2,128)(2,1)}, u32[]{:S(2)}, u32[]{:S(2)}) async-start(bf16[48,1,2,1280]{3,2,1,0:T(2,128)(2,1)} %bitcast.86), calls=%async_computation.5 | async-start | bytes 491520 | tf_op jit(solution)/shard_map/all_to_all | solution.py:90
  150.8 155.2 %all-reduce.2.cloned.1.call-start = ((), (), s32[]{:S(2)}) async-start(), calls=%async_computation.10 | async-start | bytes 163840 | tf_op jit(solution)/shard_map/psum | solution.py:117
  168.3 5.6 %copy-start.5 = (bf16[1280,16]{0,1:T(8,128)(2,1)S(1)}, bf16[1280,16]{0,1:T(8,128)(2,1)}, u32[]{:S(2)}) copy-start(bf16[1280,16]{0,1:T(8,128)(2,1)} %param.9) | copy-start | bytes 122884
  168.3 5.6 %copy-start.7 = (f32[1280]{0:T(1024)S(1)}, f32[1280]{0:T(1024)}, u32[]{:S(2)}) copy-start(f32[1280]{0:T(1024)} %param.8) | copy-start | bytes 15364
Sparse Core Ops, SparseCore 0:
  75.6 19.4 reduce-scatter.2
  98.0 19.6 reduce-scatter.4
  184.7 121.1 all-reduce.1
where the time goes:
time: 317 us; the launch traced here: 314 us
  blocking collectives  93.6 us (30%)
  waiting for transfers between devices  73.9 us (23%)
  matrix products  56.6 us (18%)
  starting transfers between devices  28 us (9%)
  local copies, waits for them, and re-layouts  27 us (9%)
  other arithmetic  21 us (7%)
  between operations  13.9 us (4%)
    psum x1, waiting for transfers between devices, local(): lax.psum((gain_term, keys_term), ('dp', 'expert', 'tensor'))  73.2 us
    psum x1, blocking collectives, local(): lax.psum((gain_term, keys_term), ('dp', 'expert', 'tensor'))  39.8 us
    all_gather x1, blocking collectives, local(): lax.all_gather(hidden, 'dp', axis=0, tiled=True)  17.8 us
    all_gather x1, blocking collectives, local(): lax.all_gather(grad_pre, 'dp', axis=0, tiled=True)  15.8 us
    all_gather x1, blocking collectives, local(): lax.all_gather(grads_sent, 'tensor', axis=0, tiled=True)  11.1 us
    dot_general x1, matrix products, mixing_backward(): jnp.einsum('bmn,dn->bmd', grad_logits, keys_wide, precision=lax.Precision...  10.6 us
    all_gather x1, blocking collectives, local(): lax.all_gather(arrived, 'tensor', axis=0, tiled=True).reshape(-1, features)  9.08 us
    convert_element_type x1, other arithmetic, local(): (cotangent.astype(jnp.float32) + grad_tok).astype(jnp.bfloat16)  8.39 us
  transfers between devices with their start and end apart: 9, of which 2 were waited for; matrix products, arithmetic and copies ran while one was open for 16% of the time, Pallas kernels for 0%

commit v1 on v0

--- a/solution.py
+++ b/solution.py
@@ -1,6 +1,9 @@
 import jax
 import jax.numpy as jnp
 from jax import lax
+from jax.experimental import pallas as pl
+from jax.experimental.pallas import tpu as pltpu
+import functools
 from jax.sharding import PartitionSpec as P
 
 SLOT_PER = 2
@@ -67,60 +70,331 @@
     )
 
 
-def local(tokens, cotangent, norm_gain, slot_keys, w_in, w_out):
+MESH = pl.DeviceIdType.MESH
+AXES = ("dp", "expert", "tensor")
+GELU_A = 0.7978845608028654
+GELU_B = 0.044715
+TILE = 256
+
+
+def gelu_of(x):
+    return 0.5 * x * (1.0 + jnp.tanh(GELU_A * (x + GELU_B * (x * x * x))))
+
+
+def gelu_slope(x):
+    square = x * x
+    bend = jnp.tanh(GELU_A * (x + GELU_B * (square * x)))
+    return 0.5 * (1.0 + bend) + 0.5 * x * (1.0 - bend * bend) * (
+        GELU_A * (1.0 + 3.0 * GELU_B * square)
+    )
+
+
+def experts_kernel(dp, experts, tensor, spread, blk, w1, w2, back, s_all, g_all, h_all, p_all,
+                   rows, s32, g32, pre, part, sent, got, pair, ret,
+                   zs, zr, ys, yr, xs, xr, ps, pr, bs, br):
+    d, e, t = (lax.axis_index(name) for name in AXES)
+    height = blk.shape[1]
+    half = height // 2
+    own = experts * half
+    group = tensor * own
+    width = blk.shape[2]
+    units = w1.shape[1]
+
+    def around(position, step, size):
+        return lax.rem(position + (step + size), size)
+
+    def push(src, dst, send, recv, axis, where):
+        target = {"dp": d, "expert": e, "tensor": t}
+        target[axis] = where
+        return pltpu.make_async_remote_copy(
+            src_ref=src, dst_ref=dst, send_sem=send, recv_sem=recv,
+            device_id=tuple(target[name] for name in AXES), device_id_type=MESH,
+        )
+
+    barrier = pltpu.get_barrier_semaphore()
+    peers = [("expert", e, experts), ("tensor", t, tensor)] + ([("dp", d, dp)] if spread > 1 else [])
+    count = 0
+    for axis, place, size in peers:
+        for k in range(1, size):
+            target = {"dp": d, "expert": e, "tensor": t}
+            target[axis] = around(place, k, size)
+            pl.semaphore_signal(barrier, inc=1, device_id=tuple(target[n] for n in AXES), device_id_type=MESH)
+            count += 1
+    pl.semaphore_wait(barrier, count)
+
+    mine = d if spread > 1 else 0
+    started = []
+
+    def launch(copy):
+        copy.start()
+        started.append(copy)
+
+    arrive = [None] * experts
+    for k in sorted(range(1, experts), key=lambda k: -min(k, experts - k)):
+        to = around(e, k, experts)
+        arrive[k] = push(blk.at[to], rows.at[mine, t, e], zs.at[k], zr.at[k], "expert", to)
+        launch(arrive[k])
+
+    def spread_y(src, k):
+        slot = rows.at[mine, t, around(e, -k, experts)]
+        for j in range(1, tensor):
+            launch(push(src, slot, ys.at[j, k], yr.at[j, k], "tensor", around(t, j, tensor)))
+
+    def spread_x(src, j, k):
+        if spread > 1:
+            slot = rows.at[mine, around(t, -j, tensor), around(e, -k, experts)]
+            for i in range(1, dp):
+                launch(push(src, slot, xs.at[j, i, k], xr.at[j, i, k], "dp", around(d, i, dp)))
+
+    spread_y(blk.at[e], 0)
+    spread_x(blk.at[e], 0, 0)
+    rows[mine, t, e] = blk[e]
+    near = sorted(range(1, experts), key=lambda k: -min(k, experts - k))
+    for k in near:
+        arrive[k].wait_recv()
+        slot = rows.at[mine, t, around(e, -k, experts)]
+        spread_y(slot, k)
+        spread_x(slot, 0, k)
+    for k in [0] + near:
+        for j in range(1, tensor):
+            slot = rows.at[mine, around(t, -j, tensor), around(e, -k, experts)]
+            push(slot, slot, ys.at[j, k], yr.at[j, k], "tensor", around(t, j, tensor)).wait_recv()
+            spread_x(slot, j, k)
+
+    def unpack(where, base):
+        count = tensor * experts
+        for n in range(count):
+            s32[pl.ds(half * n, height), :] = rows[where, n // experts, n % experts].astype(jnp.float32)
+        lead = (-half) % 8
+        for n in reversed(range(count)):
+            g32[pl.ds(half * n + lead, height), :] = rows[where, n // experts, n % experts].astype(jnp.float32)
+        s_all[pl.ds(base, group), :] = s32[0:group, :].astype(jnp.bfloat16)
+        g_all[pl.ds(base, group), :] = g32[half + lead:half + lead + group, :].astype(jnp.bfloat16)
+
+    def forward(base):
+        @pl.loop(0, units // TILE)
+        def _(n):
+            cols = pl.ds(pl.multiple_of(n * TILE, TILE), TILE)
+            x = jnp.dot(s_all[pl.ds(base, group), :], w1[:, cols], preferred_element_type=jnp.float32)
+            pre[:, cols] = x
+            h_all[pl.ds(base, group), cols] = gelu_of(x).astype(jnp.bfloat16)
+
+    def backward(base):
+        @pl.loop(0, units // TILE)
+        def _(n):
+            cols = pl.ds(pl.multiple_of(n * TILE, TILE), TILE)
+            x = contract_cols(g_all[pl.ds(base, group), :], w2[cols, :])
+            p_all[pl.ds(base, group), cols] = (x * gelu_slope(pre[:, cols])).astype(jnp.bfloat16)
+
+    def share(which):
+        for j in range(1, tensor):
+            to = around(t, j, tensor)
+            sent[which, j - 1] = part[which, pl.ds(pl.multiple_of(to * own, 8), own), :].astype(jnp.bfloat16)
+            launch(push(sent.at[which, j - 1], got.at[which, j - 1], ps.at[which, j], pr.at[which, j], "tensor", to))
+
+    base = 0
+    unpack(mine, base)
+    forward(base)
+
+    @pl.loop(0, width // TILE)
+    def _(n):
+        cols = pl.ds(pl.multiple_of(n * TILE, TILE), TILE)
+        part[0, :, cols] = jnp.dot(h_all[0:group, :], w2[:, cols], preferred_element_type=jnp.float32)
+
+    share(0)
+    backward(base)
+
+    @pl.loop(0, width // TILE)
+    def _(n):
+        cols = pl.ds(pl.multiple_of(n * TILE, TILE), TILE)
+        part[1, :, cols] = contract_cols(p_all[0:group, :], w1[cols, :])
+
+    share(1)
+    for which in range(2):
+        total = part[which, pl.ds(pl.multiple_of(t * own, 8), own), :]
+        for j in range(1, tensor):
+            push(got.at[which, j - 1], got.at[which, j - 1], ps.at[which, j], pr.at[which, j],
+                 "tensor", around(t, j, tensor)).wait_recv()
+            total = total + got[which, j - 1].astype(jnp.float32)
+        (s32 if which == 0 else g32)[0:own, :] = total
+    for n in range(experts):
+        pair[0:half, :] = s32[half * n:half * n + half, :]
+        pair[half:height, :] = g32[half * n:half * n + half, :]
+        ret[n] = pair[...].astype(jnp.bfloat16)
+    backs = []
+    for k in near:
+        to = around(e, k, experts)
+        backs.append(push(ret.at[to], back.at[e], bs.at[k], br.at[k], "expert", to))
+        launch(backs[-1])
+    back[e] = ret[e]
+    if spread > 1:
+        for i in range(1, dp):
+            other = around(d, -i, dp)
+            for j in range(tensor):
+                for k in range(experts):
+                    slot = rows.at[other, around(t, -j, tensor), around(e, -k, experts)]
+                    push(slot, slot, xs.at[j, i, k], xr.at[j, i, k], "dp", around(d, i, dp)).wait_recv()
+            unpack(other, i * group)
+            forward(i * group)
+            backward(i * group)
+    for copy in backs:
+        copy.wait_recv()
+    for copy in started:
+        copy.wait_send()
+
+
+def run_experts(blk, w1, w2, dp, experts, tensor):
+    height, width = blk.shape[1:]
+    units = w1.shape[1]
+    spread = dp if dp <= 2 else 1
+    group = tensor * experts * (height // 2)
+    own = experts * (height // 2)
+    total = spread * group
+    low, wide = jnp.bfloat16, jnp.float32
+    dma = pltpu.SemaphoreType.DMA
+    vm = pl.BlockSpec(memory_space=pltpu.VMEM)
+    return pl.pallas_call(
+        functools.partial(experts_kernel, dp, experts, tensor, spread),
+        out_shape=(
+            jax.ShapeDtypeStruct(blk.shape, low),
+            jax.ShapeDtypeStruct((total, width), low),
+            jax.ShapeDtypeStruct((total, width), low),
+            jax.ShapeDtypeStruct((total, units), low),
+            jax.ShapeDtypeStruct((total, units), low),
+        ),
+        in_specs=[vm] * 3,
+        out_specs=[vm] * 5,
+        scratch_shapes=[
+            pltpu.VMEM((spread, tensor, experts, height, width), low),
+            pltpu.VMEM((group + 2 * height, width), wide),
+            pltpu.VMEM((group + 2 * height, width), wide),
+            pltpu.VMEM((group, units), wide),
+            pltpu.VMEM((2, group, width), wide),
+            pltpu.VMEM((2, max(tensor - 1, 1), own, width), low),
+            pltpu.VMEM((2, max(tensor - 1, 1), own, width), low),
+            pltpu.VMEM((height, width), wide),
+            pltpu.VMEM((experts, height, width), low),
+            dma((experts,)), dma((experts,)),
+            dma((tensor, experts)), dma((tensor, experts)),
+            dma((tensor, dp, experts)), dma((tensor, dp, experts)),
+            dma((2, tensor)), dma((2, tensor)),
+            dma((experts,)), dma((experts,)),
+        ],
+        compiler_params=pltpu.CompilerParams(
+            collective_id=0, has_side_effects=True, vmem_limit_bytes=60 * 1024 * 1024
+        ),
+        name="experts",
+    )(blk, w1, w2)
+
+
+def reduce_kernel(sizes, x, out, got, total, ss, sr, gs, gr):
+    where = [lax.axis_index(name) for name in AXES]
+    count = sizes[0] * sizes[1] * sizes[2]
+    me = (where[0] * sizes[1] + where[1]) * sizes[2] + where[2]
+
+    def device(index):
+        return (index // (sizes[1] * sizes[2]), (index // sizes[2]) % sizes[1], index % sizes[2])
+
+    def later(k):
+        return lax.rem(me + k, count)
+
+    def scatter(k):
+        to = later(k)
+        return pltpu.make_async_remote_copy(
+            src_ref=x.at[to], dst_ref=got.at[k], send_sem=ss.at[k], recv_sem=sr.at[k],
+            device_id=device(to), device_id_type=MESH)
+
+    def gather(k):
+        to = later(k)
+        return pltpu.make_async_remote_copy(
+            src_ref=total, dst_ref=out.at[me], send_sem=gs.at[k], recv_sem=gr.at[k],
+            device_id=device(to), device_id_type=MESH)
+
+    def each(body):
+        def step(k, carry):
+            body(k)
+            return carry
+        lax.fori_loop(1, count, step, 0)
+
+    barrier = pltpu.get_barrier_semaphore()
+    each(lambda k: pl.semaphore_signal(barrier, inc=1, device_id=device(later(k)), device_id_type=MESH))
+    pl.semaphore_wait(barrier, count - 1)
+    each(lambda k: scatter(k).start())
+    got[0] = x[me]
+    each(lambda k: scatter(k).wait_recv())
+    total[...] = jnp.sum(got[...], axis=0)
+    each(lambda k: gather(k).start())
+    out[me] = total[...]
+    each(lambda k: gather(k).wait_recv())
+    each(lambda k: scatter(k).wait_send())
+    each(lambda k: gather(k).wait_send())
+
+
+def reduce_all(values, sizes):
+    count = sizes[0] * sizes[1] * sizes[2]
+    flat = jnp.concatenate([v.reshape(-1) for v in values])
+    chunk = -(-flat.shape[0] // (count * 1024)) * 1024
+    packed = jnp.pad(flat, (0, count * chunk - flat.shape[0])).reshape(count, chunk // 128, 128)
+    vm = pl.BlockSpec(memory_space=pltpu.VMEM)
+    dma = pltpu.SemaphoreType.DMA
+    summed = pl.pallas_call(
+        functools.partial(reduce_kernel, sizes),
+        out_shape=jax.ShapeDtypeStruct(packed.shape, jnp.float32),
+        in_specs=[vm],
+        out_specs=vm,
+        scratch_shapes=[
+            pltpu.VMEM(packed.shape, jnp.float32),
+            pltpu.VMEM(packed.shape[1:], jnp.float32),
+            dma((count,)), dma((count,)), dma((count,)), dma((count,)),
+        ],
+        compiler_params=pltpu.CompilerParams(collective_id=1, has_side_effects=True),
+        name="reduce",
+    )(packed).reshape(-1)
+    results, start = [], 0
+    for v in values:
+        results.append(summed[start:start + v.size].reshape(v.shape))
+        start += v.size
+    return results
+
+
+def local(sizes, tokens, cotangent, norm_gain, slot_keys, w_in, w_out):
+    dp, experts, tensor = sizes
     local_imgs, token_count, features = tokens.shape
     slot_count = slot_keys.shape[1]
-    experts = slot_count // SLOT_PER
     slot_values, combine, saved = mixing_forward(tokens, norm_gain, slot_keys)
-    slot_inputs = slot_values.astype(jnp.bfloat16).reshape(local_imgs, experts, SLOT_PER, features)
-    arrived = lax.all_to_all(slot_inputs, "expert", split_axis=1, concat_axis=0, tiled=True)
-    slot_rows = lax.all_gather(arrived, "tensor", axis=0, tiled=True).reshape(-1, features)
-    first_proj = w_in[0]
-    second_proj = w_out[0]
-    pre_act = jnp.dot(slot_rows, first_proj, preferred_element_type=jnp.float32)
-    hidden = jax.nn.gelu(pre_act).astype(jnp.bfloat16)
-    segment = hidden
-    outputs = lax.psum_scatter(
-        jnp.dot(segment, second_proj, preferred_element_type=jnp.float32),
-        "tensor",
-        scatter_dimension=0,
-        tiled=True,
-    )
-    outputs = outputs.astype(jnp.bfloat16).reshape(arrived.shape)
-    returned = lax.all_to_all(outputs, "expert", split_axis=0, concat_axis=1, tiled=True).reshape(
-        local_imgs, slot_count, features
-    )
     combine_low = combine.astype(jnp.bfloat16)
     grad_slots = jnp.einsum(
         "bmn,bmd->bnd", combine_low, cotangent, preferred_element_type=jnp.float32
     )
-    grad_slots = grad_slots.astype(jnp.bfloat16).reshape(local_imgs, experts, SLOT_PER, features)
+    both = jnp.stack([slot_values.astype(jnp.bfloat16), grad_slots.astype(jnp.bfloat16)])
+    both = both.reshape(2, local_imgs, experts, SLOT_PER, features)
+    blk = both.transpose(2, 0, 1, 3, 4).reshape(experts, 2 * local_imgs * SLOT_PER, features)
+    back, slot_rows, grad_rows, hidden, grad_pre = run_experts(
+        blk, w_in[0], w_out[0], dp, experts, tensor
+    )
+    back = back.reshape(experts, 2, local_imgs, SLOT_PER, features).transpose(1, 2, 0, 3, 4)
+    back = back.reshape(2, local_imgs, slot_count, features)
+    returned, grad_back = back[0], back[1]
+    if dp > 2:
+        slot_rows = lax.all_to_all(slot_rows, "dp", split_axis=1, concat_axis=0, tiled=True)
+        grad_rows = lax.all_to_all(grad_rows, "dp", split_axis=1, concat_axis=0, tiled=True)
+        hidden = lax.all_gather(hidden, "dp", axis=0, tiled=True)
+        grad_pre = lax.all_gather(grad_pre, "dp", axis=0, tiled=True)
+    else:
+        width = features // dp
+        start = lax.axis_index("dp") * width
+        slot_rows = lax.dynamic_slice_in_dim(slot_rows, start, width, axis=1)
+        grad_rows = lax.dynamic_slice_in_dim(grad_rows, start, width, axis=1)
+    first_total = contract_rows(slot_rows, grad_pre)
+    second_total = contract_rows(hidden, grad_rows)
     grad_combine = jnp.einsum(
         "bmd,bnd->bmn", cotangent, returned, preferred_element_type=jnp.float32
     )
-    grads_sent = lax.all_to_all(grad_slots, "expert", split_axis=1, concat_axis=0, tiled=True)
-    grad_rows = lax.all_gather(grads_sent, "tensor", axis=0, tiled=True).reshape(-1, features)
-    grad_hidden = contract_cols(grad_rows, second_proj)
-    grad_pre = jax.vjp(jax.nn.gelu, pre_act)[1](grad_hidden)[0].astype(jnp.bfloat16)
-    segment = grad_pre
-    grad_in_rows = lax.psum_scatter(
-        contract_cols(segment, first_proj), "tensor", scatter_dimension=0, tiled=True
-    )
-    grad_in_rows = grad_in_rows.astype(jnp.bfloat16).reshape(arrived.shape)
-    grad_back = lax.all_to_all(
-        grad_in_rows, "expert", split_axis=0, concat_axis=1, tiled=True
-    ).reshape(local_imgs, slot_count, features)
     grad_tok, gain_term, keys_term = mixing_backward(
         saved, norm_gain, slot_keys, grad_back, grad_combine
     )
     grad_tokens = (cotangent.astype(jnp.float32) + grad_tok).astype(jnp.bfloat16)
-    grad_gain, grad_keys = lax.psum((gain_term, keys_term), ("dp", "expert", "tensor"))
-    split_rows, split_grads = (
-        lax.all_to_all(slot_rows, "dp", split_axis=1, concat_axis=0, tiled=True),
-        lax.all_to_all(grad_rows, "dp", split_axis=1, concat_axis=0, tiled=True),
-    )
-    first_total = contract_rows(split_rows, lax.all_gather(grad_pre, "dp", axis=0, tiled=True))
-    second_total = contract_rows(lax.all_gather(hidden, "dp", axis=0, tiled=True), split_grads)
+    grad_gain, grad_keys = reduce_all((gain_term, keys_term), sizes)
     return (
         grad_tokens,
         grad_gain,
@@ -140,7 +414,7 @@
         P("expert", "tensor", None),
     )
     return jax.shard_map(
-        local,
+        functools.partial(local, tuple(mesh.shape[name] for name in AXES)),
         mesh=mesh,
         in_specs=placed,
         out_specs=(

time: 317 us -> 134 us (0.42)
  blocking collectives: 93.6 us -> 0 us
  waiting for transfers between devices: 73.9 us -> 0 us
  Pallas kernels: 0 us -> 73.1 us
  starting transfers between devices: 28 us -> 0 us
  local copies, waits for them, and re-layouts: 27 us -> 6.91 us
  matrix products: 56.6 us -> 39.1 us
  between operations: 13.9 us -> 0.93 us
  other arithmetic: 21 us -> 13.4 us
    psum x1 -> x0, waiting for transfers between devices: 73.2 us -> none  [local(): lax.psum((gain_term, keys_term), ('dp', 'expert', 'tensor'))]
    pallas_call x0 -> x2, Pallas kernels: none -> 73.1 us  [the longest x1 54.3 us: run_experts(): pl.pallas_call(functools.partial(experts_kernel, dp, experts, tensor, spr...]
    all_gather x4 -> x0, blocking collectives: 53.8 us -> none  [the longest x1 17.8 us: local(): lax.all_gather(hidden, 'dp', axis=0, tiled=True)]
    psum x1 -> x0, blocking collectives: 39.8 us -> none  [local(): lax.psum((gain_term, keys_term), ('dp', 'expert', 'tensor'))]
    all_to_all x6 -> x0, starting transfers between devices: 27.9 us -> none  [the longest x1 6.35 us: local(): lax.all_to_all(slot_inputs, 'expert', split_axis=1, concat_axis=0, tiled=...]
    dot_general x4 -> x0, matrix products: 12.2 us -> none  [the longest x2 5.66 us: contract_cols(): lax.dot_general(left, right, (((1,), (1,)), ((), ())), preferred_element_...]
    reshape x10 -> x3, local copies, waits for them, and re-layouts: 14 us -> 2.4 us  [the longest x1 1.22 us: local(): back.reshape(experts, 2, local_imgs, SLOT_PER, features)]
    all_to_all x6 -> x0, local copies, waits for them, and re-layouts: 10.7 us -> none  [the longest x2 4 us: local(): lax.all_to_all(slot_rows, 'dp', split_axis=1, concat_axis=0, tiled=True)]
  transfers between devices with their start and end apart: 9 -> 0, of which waited for: 2 -> 0; matrix products, arithmetic and copies ran while one was open for 16% -> 0% of each run, Pallas kernels for 0% -> 0%
where the time goes in v1:
time: 134 us; the launch traced here: 133 us
  Pallas kernels  73.1 us (55%)
  matrix products  39.1 us (29%)
  other arithmetic  13.4 us (10%)
  local copies, waits for them, and re-layouts  6.91 us (5%)
    pallas_call x1, Pallas kernels, run_experts(): pl.pallas_call(functools.partial(experts_kernel, dp, experts, tensor, spr...  54.3 us
    pallas_call x1, Pallas kernels, reduce_all(): pl.pallas_call(functools.partial(reduce_kernel, sizes), out_shape=jax.Sha...  18.8 us
    dot_general x1, matrix products, mixing_backward(): jnp.einsum('bmn,dn->bmd', grad_logits, keys_wide, precision=lax.Precision...  9.19 us
    dot_general x2, matrix products, contract_rows(): lax.dot_general(left, right, (((0,), (0,)), ((), ())), preferred_element_...  5.87 us
    dot_general x1, matrix products, mixing_backward(): jnp.einsum('bmd,bmn->dn', normed.astype(jnp.float32), grad_logits, precis...  5 us
    convert_element_type x1, other arithmetic, local(): (cotangent.astype(jnp.float32) + grad_tok).astype(jnp.bfloat16)  4.73 us
    dot_general x1, matrix products, mixing_backward(): jnp.einsum('bmn,bnd->bmd', dispatch_low, slot_grad, preferred_element_typ...  4.39 us
    dot_general x1, matrix products, mixing_backward(): jnp.einsum('bnd,bmd->bmn', slot_grad, normed, preferred_element_type=jnp....  3.56 us

profile of v1, /device:TPU:0, one launch (start us, length us, event | category | flops | bytes accessed | tf_op | source)
XLA Modules:
  0.0 133.5 jit_solution(12189314069016100089)
XLA Ops:
  0.7 2.8 %convert_reduce_fusion = f32[6,256]{1,0:T(8,128)S(1)} fusion(bf16[6,256,1280]{2,1,0:T(8,128)(2,1)} %param.6), kind=kLoop, calls=%fused_computation.3 | loop fusion | flops 3930624 | bytes 3938304 | tf_op jit(solution)/shard_map/reduce_sum | solution.py:16
  3.5 3.3 %fusion.15 = f32[6,256]{1,0:T(8,128)S(1)} fusion(bf16[6,256,1280]{2,1,0:T(8,128)(2,1)} %param.6, f32[6,256]{1,0:T(8,128)S(1)} %broadcast_multiply_fusion.2), kind=kLoop, calls=%fused_computation.17 | loop fusion | flops 7862784 | bytes 3944448 | tf_op jit(solution)/shard_map/reduce_sum | solution.py:18
  6.9 1.6 %fusion.27 = f32[6,256,16]{1,2,0:T(8,128)S(1)} fusion(bf16[1280,16]{0,1:T(8,128)(2,1)S(1)} %copy-done, bf16[6,256,1280]{2,1,0:T(8,128)(2,1)S(1)} %copy-done.1, f32[1280]{0:T(1024)S(1)} %copy-done.7, f32[6,256]{1,0:T(8,128)S(1)} %add_rsqrt_fusion, f32[6,256]{1,0:T(8,128)S(1)} %broadcast_multiply_fusion.2), kind=kOutput, calls=%fused_computation.46 | convolution fusion | flops 72744960 | bytes 4088832 | tf_op jit(solution)/shard_map/bmd,dn->bmn/dot_general | solution.py:22
  8.5 1.0 fusion.41
  9.5 0.4 fusion.40
  9.9 2.7 %convolution_convert_fusion.2 = bf16[6,16,1280]{2,1,0:T(8,128)(2,1)S(1)} fusion(bf16[6,256,1280]{2,1,0:T(8,128)(2,1)} %param.7, f32[6,256]{1,0:T(8,128)S(1)} %get-tuple-element.25, f32[6,256,16]{1,2,0:T(8,128)S(1)} %fusion.27), kind=kOutput, calls=%fused_computation.25 | convolution fusion | flops 63112720 | bytes 4282368 | tf_op jit(solution)/shard_map/bmn,bmd->bnd/dot_general | solution.py:366
  12.6 0.1 stack.10
  12.7 3.5 %convolution_convert_fusion.3 = bf16[6,16,1280]{2,1,0:T(8,128)(2,1)S(1)} fusion(f32[6,16]{1,0:T(8,128)S(1)} %get-tuple-element.27, f32[6,256,16]{1,2,0:T(8,128)S(1)} %fusion.27, bf16[6,256,1280]{2,1,0:T(8,128)(2,1)} %param.6, f32[1280]{0:T(1024)S(1)} %copy-done.7, f32[6,256]{1,0:T(8,128)S(1)} %add_rsqrt_fusion, f32[6,256]{1,0:T(8,128)S(1)} %broadcast_multiply_fusion.2), kind=kOutput, calls=%fused_computation.26 | convolution fusion | flops 72941920 | bytes 4294016 | tf_op jit(solution)/shard_map/bmn,bmd->bnd/dot_general | solution.py:26
  16.2 0.1 stack.9
  16.3 0.4 copy_bitcast_fusion
  16.7 1.0 reshape.65.blk
  17.7 54.3 %experts.1 = (bf16[8,24,1280]{2,1,0:T(8,128)(2,1)}, bf16[384,1280]{1,0:T(8,128)(2,1)}, bf16[384,1280]{1,0:T(8,128)(2,1)}, bf16[384,1280]{1,0:T(8,128)(2,1)}, bf16[384,1280]{1,0:T(8,128)(2,1)}) custom-call(bf16[8,24,1280]{2,1,0:T(8,128)(2,1)} %reshape.65.blk, bf16[1280,1280]{1,0:T(8,128)(2,1)} %bitcast.37, bf16[1280,1280]{1,0:T(8,128)(2,1)} %bitcast.38), custom_call_target="tpu_custom_call" | custom-call | tf_op jit(solution)/shard_map/experts/pallas_call | solution.py:256
  72.0 1.2 reshape.66
  73.2 0.3 fusion.39
  73.6 0.2 copy.19
  73.7 0.1 squeeze.15
  73.8 3.3 %multiply_reduce_fusion.1 = (f32[6,256]{1,0:T(8,128)S(1)}, f32[6,256,16]{1,2,0:T(8,128)S(1)}) fusion(f32[6,256,16]{1,2,0:T(8,128)S(1)} %get-tuple-element.26, f32[6,256]{1,0:T(8,128)S(1)} %get-tuple-element.25, bf16[6,16,1280]{2,1,0:T(8,128)(2,1)S(1)} %squeeze.15, bf16[6,256,1280]{2,1,0:T(8,128)(2,1)} %param.7), kind=kOutput, calls=%fused_computation.40 | convolution fusion | flops 62986752 | bytes 4386816 | tf_op jit(solution)/shard_map/bmd,bnd->bmn/dot_general | solution.py:390
  77.1 0.2 copy.18
  77.4 3.6 %multiply_reduce_fusion.2 = (f32[6,16]{1,0:T(8,128)S(1)}, f32[6,256,16]{1,2,0:T(8,128)S(1)}) fusion(f32[6,256,16]{1,2,0:T(8,128)S(1)} %get-tuple-element.28, f32[6,16]{1,0:T(8,128)S(1)} %get-tuple-element.27, bf16[6,16,1280]{2,1,0:T(8,128)(2,1)S(1)} %squeeze.14, bf16[6,256,1280]{2,1,0:T(8,128)(2,1)} %param.6, f32[1280]{0:T(1024)S(1)} %copy-done.7, ...), kind=kOutput, calls=%fused_computation.41 | convolution fusion | flops 72818592 | bytes 4392704 | tf_op jit(solution)/shard_map/bnd,bmd->bmn/dot_general | solution.py:34
  81.0 0.1 multiply_add_fusion
  81.1 5.0 %convolution_bitcast_fusion = f32[1280,16]{1,0:T(8,128)S(1)} fusion(f32[6,256,16]{1,2,0:T(8,128)S(1)} %multiply_add_fusion, bf16[6,256,1280]{2,1,0:T(8,128)(2,1)S(1)} %copy-done.2, f32[1280]{0:T(1024)S(1)} %copy-done.7, f32[6,256]{1,0:T(8,128)S(1)} %add_rsqrt_fusion, f32[6,256]{1,0:T(8,128)S(1)} %broadcast_multiply_fusion.2), kind=kOutput, calls=%fused_computation.24 | convolution fusion | flops 387317760 | bytes 4129792 | tf_op jit(solution)/shard_map/bmd,bmn->dn/dot_general | solution.py:50
  86.1 0.2 reshape.67
  86.3 2.2 %fusion.16 = bf16[1,640,1280]{2,1,0:T(8,128)(2,1)} fusion(bf16[384,1280]{1,0:T(8,128)(2,1)S(1)} %copy-done.5, bf16[384,1280]{1,0:T(8,128)(2,1)S(1)} %copy-done.6, s32[]{:T(128)S(6)} %select_n.4), kind=kOutput, calls=%fused_computation.22 | convolution fusion | flops 629964800 | bytes 3112964 | tf_op jit(solution)/shard_map/dot_general | solution.py:62
  88.6 3.6 %fusion.17 = bf16[1,1280,640]{2,1,0:T(8,128)(2,1)} fusion(bf16[384,1280]{1,0:T(8,128)(2,1)} %get-tuple-element.13, bf16[384,1280]{1,0:T(8,128)(2,1)} %get-tuple-element.14, s32[]{:T(128)S(6)} %select_n.4), kind=kOutput, calls=%fused_computation.23 | convolution fusion | flops 629964800 | bytes 3112964 | tf_op jit(solution)/shard_map/dot_general | solution.py:62
  92.2 4.4 %fusion.29 = f32[6,256,1280]{2,1,0:T(8,128)} fusion(bf16[6,16,1280]{2,1,0:T(8,128)(2,1)S(1)} %squeeze.14, f32[6,16]{1,0:T(8,128)S(1)} %get-tuple-element.27, f32[6,256,16]{1,2,0:T(8,128)S(1)} %fusion.27), kind=kOutput, calls=%fused_computation.48 | convolution fusion | flops 62988640 | bytes 8208768 | tf_op jit(solution)/shard_map/bmn,bnd->bmd/dot_general | solution.py:37
  96.6 9.2 %fusion.14 = (f32[1280]{0:T(1024)S(1)}, f32[6,256]{1,0:T(8,128)S(1)}, f32[6,256]{1,0:T(8,128)S(1)}, f32[6,256,1280]{2,1,0:T(8,128)S(1)}) fusion(bf16[6,256,1280]{2,1,0:T(8,128)(2,1)} %param.6, f32[6,256]{1,0:T(8,128)S(1)} %add_rsqrt_fusion, f32[6,256]{1,0:T(8,128)S(1)} %broadcast_multiply_fusion.2, f32[1280]{0:T(1024)S(1)} %copy-done.7, ...), kind=kOutput, calls=%fused_computation.16 | convolution fusion | flops 397143808 | bytes 19834880 | tf_op jit(solution)/shard_map/bmn,dn->bmd/dot_general | solution.py:47
  105.8 4.7 %fusion.13 = bf16[6,256,1280]{2,1,0:T(8,128)(2,1)} fusion(bf16[6,256,1280]{2,1,0:T(8,128)(2,1)S(1)} %copy-done.3, bf16[6,256,1280]{2,1,0:T(8,128)(2,1)S(1)} %copy-done.4, f32[6,256,1280]{2,1,0:T(8,128)S(1)} %get-tuple-element.33, f32[6,256]{1,0:T(8,128)S(1)} %get-tuple-element.34, f32[6,256]{1,0:T(8,128)S(1)} %get-tuple-element.35, f32[1280]{0:T(1024)S(1)} %copy-done.7, ...), kind=kLoop, calls=%fused_computation.15 | loop fusion | flops 21626880 | bytes 19690496 | tf_op jit(solution)/shard_map/convert_element_type | solution.py:396
  110.6 0.6 fusion.24.x
  111.2 18.8 %reduce.1 = f32[32,8,128]{2,1,0:T(8,128)} custom-call(f32[32,8,128]{2,1,0:T(8,128)} %fusion.24.x), custom_call_target="tpu_custom_call" | custom-call | tf_op jit(solution)/shard_map/reduce/pallas_call | solution.py:340
  130.1 1.3 slice.24
  131.4 1.2 slice.20
  132.6 0.8 copy.21
  (21 shorter events, 0.2 us)
Async XLA Ops:
  0.6 6.2 %copy-start = (bf16[1280,16]{0,1:T(8,128)(2,1)S(1)}, bf16[1280,16]{0,1:T(8,128)(2,1)}, u32[]{:S(2)}) copy-start(bf16[1280,16]{0,1:T(8,128)(2,1)} %param.9) | copy-start | bytes 122884
  0.6 6.2 %copy-start.7 = (f32[1280]{0:T(1024)S(1)}, f32[1280]{0:T(1024)}, u32[]{:S(2)}) copy-start(f32[1280]{0:T(1024)} %param.8) | copy-start | bytes 15364
  0.7 6.2 %copy-start.1 = (bf16[6,256,1280]{2,1,0:T(8,128)(2,1)S(1)}, bf16[6,256,1280]{2,1,0:T(8,128)(2,1)}, u32[]{:S(2)}) copy-start(bf16[6,256,1280]{2,1,0:T(8,128)(2,1)} %param.6) | copy-start | bytes 11796484
  77.4 3.7 %copy-start.2 = (bf16[6,256,1280]{2,1,0:T(8,128)(2,1)S(1)}, bf16[6,256,1280]{2,1,0:T(8,128)(2,1)}, u32[]{:S(2)}) copy-start(bf16[6,256,1280]{2,1,0:T(8,128)(2,1)} %param.6) | copy-start | bytes 11796484
  77.4 8.9 %copy-start.5 = (bf16[384,1280]{1,0:T(8,128)(2,1)S(1)}, bf16[384,1280]{1,0:T(8,128)(2,1)}, u32[]{:S(2)}) copy-start(bf16[384,1280]{1,0:T(8,128)(2,1)} %get-tuple-element.12) | copy-start | bytes 2949124
  77.4 8.9 %copy-start.6 = (bf16[384,1280]{1,0:T(8,128)(2,1)S(1)}, bf16[384,1280]{1,0:T(8,128)(2,1)}, u32[]{:S(2)}) copy-start(bf16[384,1280]{1,0:T(8,128)(2,1)} %get-tuple-element.11) | copy-start | bytes 2949124
  96.6 9.2 %copy-start.3 = (bf16[6,256,1280]{2,1,0:T(8,128)(2,1)S(1)}, bf16[6,256,1280]{2,1,0:T(8,128)(2,1)}, u32[]{:S(2)}) copy-start(bf16[6,256,1280]{2,1,0:T(8,128)(2,1)} %param.6) | copy-start | bytes 11796484
  96.6 9.2 %copy-start.4 = (bf16[6,256,1280]{2,1,0:T(8,128)(2,1)S(1)}, bf16[6,256,1280]{2,1,0:T(8,128)(2,1)}, u32[]{:S(2)}) copy-start(bf16[6,256,1280]{2,1,0:T(8,128)(2,1)} %param.7) | copy-start | bytes 11796484

commit v2 on v1

--- a/solution.py
+++ b/solution.py
@@ -4,6 +4,7 @@
 from jax.experimental import pallas as pl
 from jax.experimental.pallas import tpu as pltpu
 import functools
+import numpy as np
 from jax.sharding import PartitionSpec as P
 
 SLOT_PER = 2
@@ -12,50 +13,176 @@
 EPSILON = 1e-06
 
 
-def mixing_forward(tokens, gain, slot_keys):
-    average = jnp.mean(tokens, axis=-1, keepdims=True, dtype=jnp.float32)
-    centred = tokens.astype(jnp.float32) - average
-    spread = jnp.mean(centred * centred, axis=-1, keepdims=True)
-    inverse = lax.rsqrt(spread + EPSILON)
-    scaled = centred * inverse
-    normed = (scaled * gain).astype(jnp.bfloat16)
-    logits = jnp.einsum("bmd,dn->bmn", normed, slot_keys, preferred_element_type=jnp.float32)
-    dispatch = jax.nn.softmax(logits, axis=1)
-    combine = jax.nn.softmax(logits, axis=2)
-    dispatch_low = dispatch.astype(jnp.bfloat16)
-    slot_values = jnp.einsum(
-        "bmn,bmd->bnd", dispatch_low, normed, preferred_element_type=jnp.float32
-    )
-    return (slot_values, combine, (scaled, inverse, normed, dispatch, combine, dispatch_low))
-
-
-def mixing_backward(saved, gain, slot_keys, slot_grad, combine_grad):
-    scaled, inverse, normed, dispatch, combine, dispatch_low = saved
-    grad_dispatch = jnp.einsum(
-        "bnd,bmd->bmn", slot_grad, normed, preferred_element_type=jnp.float32
-    )
-    grad_normed = jnp.einsum(
-        "bmn,bnd->bmd", dispatch_low, slot_grad, preferred_element_type=jnp.float32
-    )
-    grad_logits = dispatch * (
+CHUNK = 64
+
+
+def mix_kernel(x, c, gain, keys, perm, normed, disp, comb, stat, blk, stack):
+    b = pl.program_id(0)
+    slots = keys.shape[0]
+    images = pl.num_programs(0)
+    gains = gain[...]
+
+    def rows_of(n, carry):
+        rows = pl.ds(pl.multiple_of(n * CHUNK, CHUNK), CHUNK)
+        values = x[0, rows, :].astype(jnp.float32)
+        average = jnp.mean(values, axis=-1, keepdims=True)
+        centred = values - average
+        inverse = lax.rsqrt(jnp.mean(centred * centred, axis=-1, keepdims=True) + EPSILON)
+        normed[0, rows, :] = (centred * inverse * gains).astype(jnp.bfloat16)
+        lane = lax.broadcasted_iota(jnp.int32, (CHUNK, stat.shape[2]), 1)
+        stat[0, rows, :] = jnp.where(lane == 0, average, inverse)
+        return carry
+
+    lax.fori_loop(0, x.shape[1] // CHUNK, rows_of, 0)
+    logits = contract_cols(keys[...], normed[0])
+    over_tokens = jnp.exp(logits - jnp.max(logits, axis=1, keepdims=True))
+    over_tokens = over_tokens / jnp.sum(over_tokens, axis=1, keepdims=True)
+    over_slots = jnp.exp(logits - jnp.max(logits, axis=0, keepdims=True))
+    over_slots = over_slots / jnp.sum(over_slots, axis=0, keepdims=True)
+    disp[0] = over_tokens
+    comb[0] = over_slots
+    start = pl.multiple_of(b * slots, slots)
+    stack[0, pl.ds(start, slots), :] = jnp.dot(
+        over_tokens.astype(jnp.bfloat16), normed[0], preferred_element_type=jnp.float32
+    ).astype(jnp.bfloat16)
+    stack[1, pl.ds(start, slots), :] = jnp.dot(
+        over_slots.astype(jnp.bfloat16), c[0], preferred_element_type=jnp.float32
+    ).astype(jnp.bfloat16)
+
+    @pl.when(b == images - 1)
+    def _():
+        height = blk.shape[1]
+        count = stack.shape[1]
+        moved = jnp.dot(perm[:, 0:count], stack[0], preferred_element_type=jnp.float32)
+        moved = moved + jnp.dot(perm[:, count:2 * count], stack[1], preferred_element_type=jnp.float32)
+        for n in range(blk.shape[0]):
+            blk[n] = moved[n * height:(n + 1) * height].astype(jnp.bfloat16)
+
+
+def placement(images, experts):
+    slots = experts * SLOT_PER
+    height = 2 * images * SLOT_PER
+    r = np.arange(experts * height)
+    e, q = r // height, r % height
+    stream, u = q // (images * SLOT_PER), q % (images * SLOT_PER)
+    return stream, u // SLOT_PER, e * SLOT_PER + u % SLOT_PER, slots
+
+
+def mix(tokens, cotangent, gain, keys, experts):
+    images, count, features = tokens.shape
+    stream, image, slot, slots = placement(images, experts)
+    perm = np.zeros((stream.size, stream.size), np.float32)
+    perm[np.arange(stream.size), stream * images * slots + image * slots + slot] = 1.0
+    height = 2 * images * SLOT_PER
+    per_image = lambda *tail: pl.BlockSpec((1,) + tail, lambda b: (b, 0, 0))
+    whole = lambda *shape: pl.BlockSpec(shape, lambda b: (0,) * len(shape))
+    low, wide = jnp.bfloat16, jnp.float32
+    return pl.pallas_call(
+        mix_kernel,
+        grid=(images,),
+        out_shape=(
+            jax.ShapeDtypeStruct(tokens.shape, low),
+            jax.ShapeDtypeStruct((images, slots, count), wide),
+            jax.ShapeDtypeStruct((images, slots, count), wide),
+            jax.ShapeDtypeStruct((images, count, 128), wide),
+            jax.ShapeDtypeStruct((experts, height, features), low),
+        ),
+        in_specs=[
+            per_image(count, features), per_image(count, features), whole(1, features),
+            whole(slots, features), whole(*perm.shape),
+        ],
+        out_specs=(
+            per_image(count, features), per_image(slots, count), per_image(slots, count),
+            per_image(count, 128), whole(experts, height, features),
+        ),
+        scratch_shapes=[pltpu.VMEM((2, images * slots, features), low)],
+        compiler_params=pltpu.CompilerParams(vmem_limit_bytes=32 * 1024 * 1024),
+        name="mix",
+    )(tokens, cotangent, gain, keys, jnp.asarray(perm, low))
+
+
+def unmix_kernel(x, c, normed, disp, comb, stat, gain, keys, sel, back, out, gain_out, keys_out,
+                 grad, gain_sum):
+    b = pl.program_id(0)
+    slots = keys.shape[0]
+    low = jnp.bfloat16
+    got = jnp.dot(sel[0], back[...], preferred_element_type=jnp.float32).astype(low)
+    returned, slot_grad = got[0:slots], got[slots:2 * slots]
+    grad_dispatch = contract_cols(slot_grad, normed[0])
+    grad_combine = contract_cols(returned, c[0])
+    dispatch, combine = disp[0], comb[0]
+    logit = dispatch * (
         grad_dispatch - jnp.sum(dispatch * grad_dispatch, axis=1, keepdims=True)
-    )
-    grad_logits = grad_logits + combine * (
-        combine_grad - jnp.sum(combine * combine_grad, axis=2, keepdims=True)
-    )
-    keys_wide = slot_keys.astype(jnp.float32)
-    grad_normed = grad_normed + jnp.einsum(
-        "bmn,dn->bmd", grad_logits, keys_wide, precision=lax.Precision.HIGHEST
-    )
-    keys_term = jnp.einsum(
-        "bmd,bmn->dn", normed.astype(jnp.float32), grad_logits, precision=lax.Precision.HIGHEST
-    )
-    gain_term = jnp.sum(grad_normed * scaled, axis=(0, 1))
-    grad_scaled = grad_normed * gain
-    first_mean = jnp.mean(grad_scaled, axis=-1, keepdims=True)
-    second_mean = jnp.mean(grad_scaled * scaled, axis=-1, keepdims=True)
-    grad_tok = inverse * (grad_scaled - first_mean - scaled * second_mean)
-    return (grad_tok, gain_term, keys_term)
+    ) + combine * (grad_combine - jnp.sum(combine * grad_combine, axis=0, keepdims=True))
+    first = logit.astype(low)
+    rest = logit - first.astype(jnp.float32)
+    second = rest.astype(low)
+    third = (rest - second.astype(jnp.float32)).astype(low)
+    key = keys[...]
+    left = jnp.concatenate([dispatch.astype(low), first, second, third], axis=0)
+    right = jnp.concatenate([slot_grad, key, key, key], axis=0)
+    grad[...] = contract_rows(left, right)
+    parts = jnp.dot(left[slots:], normed[0], preferred_element_type=jnp.float32)
+    keys_here = parts[0:slots] + parts[slots:2 * slots] + parts[2 * slots:3 * slots]
+
+    @pl.when(b == 0)
+    def _():
+        keys_out[...] = jnp.zeros_like(keys_out)
+        gain_sum[...] = jnp.zeros_like(gain_sum)
+
+    keys_out[...] += keys_here
+    gains = gain[...]
+
+    def rows_of(n, total):
+        rows = pl.ds(pl.multiple_of(n * CHUNK, CHUNK), CHUNK)
+        average, inverse = stat[0, rows, 0:1], stat[0, rows, 1:2]
+        scaled = (x[0, rows, :].astype(jnp.float32) - average) * inverse
+        grads = grad[rows, :]
+        product = grads * scaled
+        total = total + sum(product[k:k + 8] for k in range(0, CHUNK, 8))
+        grads = grads * gains
+        first_mean = jnp.mean(grads, axis=-1, keepdims=True)
+        second_mean = jnp.mean(product * gains, axis=-1, keepdims=True)
+        change = inverse * (grads - first_mean - scaled * second_mean)
+        out[0, rows, :] = (c[0, rows, :].astype(jnp.float32) + change).astype(low)
+        return total
+
+    gain_sum[...] = lax.fori_loop(0, x.shape[1] // CHUNK, rows_of, gain_sum[...])
+
+    @pl.when(b == pl.num_programs(0) - 1)
+    def _():
+        gain_out[...] = jnp.sum(gain_sum[...], axis=0, keepdims=True)
+
+
+def unmix(tokens, cotangent, saved, gain, keys, back, experts):
+    images, count, features = tokens.shape
+    stream, image, slot, slots = placement(images, experts)
+    sel = np.zeros((images, 2 * slots, stream.size), np.float32)
+    sel[image, stream * slots + slot, np.arange(stream.size)] = 1.0
+    normed, disp, comb, stat = saved
+    per_image = lambda *tail: pl.BlockSpec((1,) + tail, lambda b: (b, 0, 0))
+    whole = lambda *shape: pl.BlockSpec(shape, lambda b: (0,) * len(shape))
+    return pl.pallas_call(
+        unmix_kernel,
+        grid=(images,),
+        out_shape=(
+            jax.ShapeDtypeStruct(tokens.shape, jnp.bfloat16),
+            jax.ShapeDtypeStruct((1, features), jnp.float32),
+            jax.ShapeDtypeStruct((slots, features), jnp.float32),
+        ),
+        in_specs=[
+            per_image(count, features), per_image(count, features), per_image(count, features),
+            per_image(slots, count), per_image(slots, count), per_image(count, 128),
+            whole(1, features), whole(slots, features),
+            per_image(2 * slots, stream.size), whole(stream.size, features),
+        ],
+        out_specs=(per_image(count, features), whole(1, features), whole(slots, features)),
+        scratch_shapes=[
+            pltpu.VMEM((count, features), jnp.float32), pltpu.VMEM((8, features), jnp.float32),
+        ],
+        compiler_params=pltpu.CompilerParams(vmem_limit_bytes=32 * 1024 * 1024),
+        name="unmix",
+    )(tokens, cotangent, normed, disp, comb, stat, gain, keys, jnp.asarray(sel, jnp.bfloat16), back)
 
 
 def contract_rows(left, right):
@@ -89,9 +216,11 @@
     )
 
 
-def experts_kernel(dp, experts, tensor, spread, blk, w1, w2, back, s_all, g_all, h_all, p_all,
-                   rows, s32, g32, pre, part, sent, got, pair, ret,
-                   zs, zr, ys, yr, xs, xr, ps, pr, bs, br):
+def experts_kernel(dp, experts, tensor, spread, finish, blk, w1, w2, back, *refs):
+    if finish:
+        grad_in, grad_out, turned, *refs = refs
+    (s_all, g_all, h_all, p_all, rows, s32, g32, pre, part, sent, got, pair, ret,
+     zs, zr, ys, yr, xs, xr, ps, pr, bs, br) = refs
     d, e, t = (lax.axis_index(name) for name in AXES)
     height = blk.shape[1]
     half = height // 2
@@ -237,6 +366,19 @@
             unpack(other, i * group)
             forward(i * group)
             backward(i * group)
+    if finish:
+        share_width = width // dp
+        mine_cols = pl.ds(pl.multiple_of(d * share_width, 128), share_width)
+        turned[...] = s_all[:, mine_cols].T
+
+        @pl.loop(0, units // TILE)
+        def _(n):
+            cols = pl.ds(pl.multiple_of(n * TILE, TILE), TILE)
+            grad_in[:, cols] = jnp.dot(
+                turned[...], p_all[:, cols], preferred_element_type=jnp.float32
+            ).astype(jnp.bfloat16)
+            grad_out[cols, :] = contract_rows(h_all[:, cols], g_all[:, mine_cols]).astype(jnp.bfloat16)
+
     for copy in backs:
         copy.wait_recv()
     for copy in started:
@@ -253,18 +395,20 @@
     low, wide = jnp.bfloat16, jnp.float32
     dma = pltpu.SemaphoreType.DMA
     vm = pl.BlockSpec(memory_space=pltpu.VMEM)
+    shapes = [(total, width), (total, width), (total, units), (total, units)]
+    finish = spread == dp and width % (128 * dp) == 0
+    kept = [pltpu.VMEM(shape, low) for shape in shapes]
+    if finish:
+        shapes = [(width // dp, units), (units, width // dp)]
+        kept = [pltpu.VMEM((width // dp, total), low)] + kept
+    else:
+        kept = []
     return pl.pallas_call(
-        functools.partial(experts_kernel, dp, experts, tensor, spread),
-        out_shape=(
-            jax.ShapeDtypeStruct(blk.shape, low),
-            jax.ShapeDtypeStruct((total, width), low),
-            jax.ShapeDtypeStruct((total, width), low),
-            jax.ShapeDtypeStruct((total, units), low),
-            jax.ShapeDtypeStruct((total, units), low),
-        ),
+        functools.partial(experts_kernel, dp, experts, tensor, spread, finish),
+        out_shape=[jax.ShapeDtypeStruct(shape, low) for shape in [blk.shape] + shapes],
         in_specs=[vm] * 3,
-        out_specs=[vm] * 5,
-        scratch_shapes=[
+        out_specs=[vm] * (1 + len(shapes)),
+        scratch_shapes=kept + [
             pltpu.VMEM((spread, tensor, experts, height, width), low),
             pltpu.VMEM((group + 2 * height, width), wide),
             pltpu.VMEM((group + 2 * height, width), wide),
@@ -289,45 +433,44 @@
 
 def reduce_kernel(sizes, x, out, got, total, ss, sr, gs, gr):
     where = [lax.axis_index(name) for name in AXES]
-    count = sizes[0] * sizes[1] * sizes[2]
-    me = (where[0] * sizes[1] + where[1]) * sizes[2] + where[2]
-
-    def device(index):
-        return (index // (sizes[1] * sizes[2]), (index // sizes[2]) % sizes[1], index % sizes[2])
-
-    def later(k):
-        return lax.rem(me + k, count)
+    table = [
+        [place] + [lax.rem(place + k, size) for k in range(1, size)]
+        for place, size in zip(where, sizes)
+    ]
+    targets = [(a, b, c) for a in table[0] for b in table[1] for c in table[2]]
+    rank = lambda p: (p[0] * sizes[1] + p[1]) * sizes[2] + p[2]
+    me = rank(where)
+    others = range(1, len(targets))
 
     def scatter(k):
-        to = later(k)
         return pltpu.make_async_remote_copy(
-            src_ref=x.at[to], dst_ref=got.at[k], send_sem=ss.at[k], recv_sem=sr.at[k],
-            device_id=device(to), device_id_type=MESH)
+            src_ref=x.at[rank(targets[k])], dst_ref=got.at[k], send_sem=ss.at[k], recv_sem=sr.at[k],
+            device_id=targets[k], device_id_type=MESH)
 
     def gather(k):
-        to = later(k)
         return pltpu.make_async_remote_copy(
             src_ref=total, dst_ref=out.at[me], send_sem=gs.at[k], recv_sem=gr.at[k],
-            device_id=device(to), device_id_type=MESH)
-
-    def each(body):
-        def step(k, carry):
-            body(k)
-            return carry
-        lax.fori_loop(1, count, step, 0)
+            device_id=targets[k], device_id_type=MESH)
 
     barrier = pltpu.get_barrier_semaphore()
-    each(lambda k: pl.semaphore_signal(barrier, inc=1, device_id=device(later(k)), device_id_type=MESH))
-    pl.semaphore_wait(barrier, count - 1)
-    each(lambda k: scatter(k).start())
+    for k in others:
+        pl.semaphore_signal(barrier, inc=1, device_id=targets[k], device_id_type=MESH)
+    pl.semaphore_wait(barrier, len(others))
+    first = [scatter(k) for k in others]
+    for copy in first:
+        copy.start()
     got[0] = x[me]
-    each(lambda k: scatter(k).wait_recv())
+    for copy in first:
+        copy.wait_recv()
     total[...] = jnp.sum(got[...], axis=0)
-    each(lambda k: gather(k).start())
+    second = [gather(k) for k in others]
+    for copy in second:
+        copy.start()
     out[me] = total[...]
-    each(lambda k: gather(k).wait_recv())
-    each(lambda k: scatter(k).wait_send())
-    each(lambda k: gather(k).wait_send())
+    for copy in second:
+        copy.wait_recv()
+    for copy in first + second:
+        copy.wait_send()
 
 
 def reduce_all(values, sizes):
@@ -359,42 +502,31 @@
 
 def local(sizes, tokens, cotangent, norm_gain, slot_keys, w_in, w_out):
     dp, experts, tensor = sizes
-    local_imgs, token_count, features = tokens.shape
-    slot_count = slot_keys.shape[1]
-    slot_values, combine, saved = mixing_forward(tokens, norm_gain, slot_keys)
-    combine_low = combine.astype(jnp.bfloat16)
-    grad_slots = jnp.einsum(
-        "bmn,bmd->bnd", combine_low, cotangent, preferred_element_type=jnp.float32
-    )
-    both = jnp.stack([slot_values.astype(jnp.bfloat16), grad_slots.astype(jnp.bfloat16)])
-    both = both.reshape(2, local_imgs, experts, SLOT_PER, features)
-    blk = both.transpose(2, 0, 1, 3, 4).reshape(experts, 2 * local_imgs * SLOT_PER, features)
-    back, slot_rows, grad_rows, hidden, grad_pre = run_experts(
-        blk, w_in[0], w_out[0], dp, experts, tensor
-    )
-    back = back.reshape(experts, 2, local_imgs, SLOT_PER, features).transpose(1, 2, 0, 3, 4)
-    back = back.reshape(2, local_imgs, slot_count, features)
-    returned, grad_back = back[0], back[1]
-    if dp > 2:
-        slot_rows = lax.all_to_all(slot_rows, "dp", split_axis=1, concat_axis=0, tiled=True)
-        grad_rows = lax.all_to_all(grad_rows, "dp", split_axis=1, concat_axis=0, tiled=True)
-        hidden = lax.all_gather(hidden, "dp", axis=0, tiled=True)
-        grad_pre = lax.all_gather(grad_pre, "dp", axis=0, tiled=True)
+    features = tokens.shape[2]
+    gain, keys = norm_gain.reshape(1, features), slot_keys.T
+    *saved, blk = mix(tokens, cotangent, gain, keys, experts)
+    back, *rest = run_experts(blk, w_in[0], w_out[0], dp, experts, tensor)
+    if len(rest) == 2:
+        first_total, second_total = rest
     else:
-        width = features // dp
-        start = lax.axis_index("dp") * width
-        slot_rows = lax.dynamic_slice_in_dim(slot_rows, start, width, axis=1)
-        grad_rows = lax.dynamic_slice_in_dim(grad_rows, start, width, axis=1)
-    first_total = contract_rows(slot_rows, grad_pre)
-    second_total = contract_rows(hidden, grad_rows)
-    grad_combine = jnp.einsum(
-        "bmd,bnd->bmn", cotangent, returned, preferred_element_type=jnp.float32
-    )
-    grad_tok, gain_term, keys_term = mixing_backward(
-        saved, norm_gain, slot_keys, grad_back, grad_combine
-    )
-    grad_tokens = (cotangent.astype(jnp.float32) + grad_tok).astype(jnp.bfloat16)
+        slot_rows, grad_rows, hidden, grad_pre = rest
+        if dp > 2:
+            slot_rows = lax.all_to_all(slot_rows, "dp", split_axis=1, concat_axis=0, tiled=True)
+            grad_rows = lax.all_to_all(grad_rows, "dp", split_axis=1, concat_axis=0, tiled=True)
+            hidden = lax.all_gather(hidden, "dp", axis=0, tiled=True)
+            grad_pre = lax.all_gather(grad_pre, "dp", axis=0, tiled=True)
+        else:
+            width = features // dp
+            start = lax.axis_index("dp") * width
+            slot_rows = lax.dynamic_slice_in_dim(slot_rows, start, width, axis=1)
+            grad_rows = lax.dynamic_slice_in_dim(grad_rows, start, width, axis=1)
+        first_total = contract_rows(slot_rows, grad_pre)
+        second_total = contract_rows(hidden, grad_rows)
+    grad_tokens, gain_term, keys_term = unmix(
+        tokens, cotangent, saved, gain, keys, back.reshape(-1, features), experts
+    )
     grad_gain, grad_keys = reduce_all((gain_term, keys_term), sizes)
+    grad_gain, grad_keys = grad_gain.reshape(features), grad_keys.T
     return (
         grad_tokens,
         grad_gain,

time: 134 us -> 129 us (0.963)
  matrix products: 39.1 us -> 0 us
  Pallas kernels: 73.1 us -> 99.1 us
  local copies, waits for them, and re-layouts: 6.91 us -> 28 us
  other arithmetic: 13.4 us -> 0.69 us
    dot_general x10 -> x0, matrix products: 39.1 us -> none  [the longest x1 9.19 us: mixing_backward(): jnp.einsum('bmn,dn->bmd', grad_logits, keys_wide, precision=lax.Precision...]
    pallas_call x0 -> x2, Pallas kernels: none -> 25.6 us  [the longest x1 13.2 us: unmix(): pl.pallas_call(unmix_kernel, grid=(images,), out_shape=(jax.ShapeDtypeStr...]
    unnamed x17 -> x42, local copies, waits for them, and re-layouts: 0.88 us -> 23.4 us
    reduce_sum x2 -> x0, other arithmetic: 6.13 us -> none  [the longest x1 3.28 us: mixing_forward(): spread = jnp.mean(centred * centred, axis=-1, keepdims=True)]
    convert_element_type x1 -> x0, other arithmetic: 4.73 us -> none  [local(): (cotangent.astype(jnp.float32) + grad_tok).astype(jnp.bfloat16)]
    sub x2 -> x0, other arithmetic: 1.37 us -> none  [the longest x1 0.97 us: mixing_forward(): dispatch = jax.nn.softmax(logits, axis=1)]
where the time goes in v2:
time: 129 us; the launch traced here: 128 us
  Pallas kernels  99.1 us (77%)
  local copies, waits for them, and re-layouts  28 us (22%)
    pallas_call x1, Pallas kernels, run_experts(): pl.pallas_call(functools.partial(experts_kernel, dp, experts, tensor, spr...  54.2 us
    unnamed x42, local copies, waits for them, and re-layouts  23.4 us
    pallas_call x1, Pallas kernels, reduce_all(): pl.pallas_call(functools.partial(reduce_kernel, sizes), out_shape=jax.Sha...  19.3 us
    pallas_call x1, Pallas kernels, unmix(): pl.pallas_call(unmix_kernel, grid=(images,), out_shape=(jax.ShapeDtypeStr...  13.2 us
    pallas_call x1, Pallas kernels, mix(): pl.pallas_call(mix_kernel, grid=(images,), out_shape=(jax.ShapeDtypeStruc...  12.3 us

profile of v2, /device:TPU:0, one launch (start us, length us, event | category | flops | bytes accessed | tf_op | source)
XLA Modules:
  0.0 128.5 jit_solution(14042274812784145703)
XLA Ops:
  0.6 0.7 reshape.31.gain
  1.3 2.1 %copy-done = bf16[6,256,1280]{2,1,0:T(8,128)(2,1)S(1)} copy-done((bf16[6,256,1280]{2,1,0:T(8,128)(2,1)S(1)}, bf16[6,256,1280]{2,1,0:T(8,128)(2,1)}, u32[]{:S(2)}) %copy-start) | copy-done | bytes 3932184
  3.4 2.1 %copy-done.2 = bf16[6,256,1280]{2,1,0:T(8,128)(2,1)S(1)} copy-done((bf16[6,256,1280]{2,1,0:T(8,128)(2,1)S(1)}, bf16[6,256,1280]{2,1,0:T(8,128)(2,1)}, u32[]{:S(2)}) %copy-start.2) | copy-done | bytes 3932184
  5.6 0.8 copy-done.10
  6.3 0.9 copy-done.17
  7.2 12.3 %mix.1 = (bf16[6,256,1280]{2,1,0:T(8,128)(2,1)S(1)}, f32[6,16,256]{2,1,0:T(8,128)S(1)}, f32[6,16,256]{2,1,0:T(8,128)S(1)}, f32[6,256,128]{2,1,0:T(8,128)S(1)}, bf16[8,24,1280]{2,1,0:T(8,128)(2,1)S(1)}) custom-call(bf16[6,256,1280]{2,1,0:T(8,128)(2,1)S(1)} %copy-done, bf16[6,256,1280]{2,1,0:T(8,128)(2,1)S(1)} %copy-done.2, f32[1,1280]{1,0:T(1,128)S(1)} %reshape.31.gain, ...), custom_call_target="tpu_custom_call" | custom-call | tf_op jit(solution)/shard_map/mix/pallas_call | solution.py:80
  19.6 0.0 copy-start.4
  19.6 1.9 %copy-done.4 = bf16[6,256,1280]{2,1,0:T(8,128)(2,1)} copy-done((bf16[6,256,1280]{2,1,0:T(8,128)(2,1)}, bf16[6,256,1280]{2,1,0:T(8,128)(2,1)S(1)}, u32[]{:S(2)}) %copy-start.4) | copy-done | bytes 3932184
  21.5 0.9 copy-done.6
  22.4 0.8 copy-done.9
  23.2 0.6 copy-done.13
  23.8 0.6 copy-done.15
  24.4 54.2 %experts.1 = (bf16[8,24,1280]{2,1,0:T(8,128)(2,1)}, bf16[640,1280]{1,0:T(8,128)(2,1)}, bf16[1280,640]{1,0:T(8,128)(2,1)}) custom-call(bf16[8,24,1280]{2,1,0:T(8,128)(2,1)} %copy-done.9, bf16[1280,1280]{1,0:T(8,128)(2,1)} %bitcast.13, bf16[1280,1280]{1,0:T(8,128)(2,1)} %bitcast.14), custom_call_target="tpu_custom_call" | custom-call | tf_op jit(solution)/shard_map/experts/pallas_call | solution.py:406
  78.7 0.0 copy-done.1
  78.7 0.0 copy-done.11
  78.7 0.0 copy-start.3
  78.7 2.1 %copy-done.3 = bf16[6,256,1280]{2,1,0:T(8,128)(2,1)S(1)} copy-done((bf16[6,256,1280]{2,1,0:T(8,128)(2,1)S(1)}, bf16[6,256,1280]{2,1,0:T(8,128)(2,1)}, u32[]{:S(2)}) %copy-start.3) | copy-done | bytes 3932184
  80.8 2.1 %copy-done.5 = bf16[6,256,1280]{2,1,0:T(8,128)(2,1)S(1)} copy-done((bf16[6,256,1280]{2,1,0:T(8,128)(2,1)S(1)}, bf16[6,256,1280]{2,1,0:T(8,128)(2,1)}, u32[]{:S(2)}) %copy-start.5) | copy-done | bytes 3932184
  83.0 1.1 copy-done.7
  84.1 1.0 copy-done.8
  85.1 0.9 copy-done.14
  86.0 0.9 copy-done.16
  86.9 13.2 %unmix.1 = (bf16[6,256,1280]{2,1,0:T(8,128)(2,1)}, f32[1,1280]{1,0:T(1,128)S(1)}, f32[16,1280]{1,0:T(8,128)S(1)}) custom-call(bf16[6,256,1280]{2,1,0:T(8,128)(2,1)S(1)} %copy-done.1, bf16[6,256,1280]{2,1,0:T(8,128)(2,1)S(1)} %copy-done.3, bf16[6,256,1280]{2,1,0:T(8,128)(2,1)S(1)} %copy-done.5, f32[6,16,256]{2,1,0:T(8,128)S(1)} %copy-done.14, ...), custom_call_target="tpu_custom_call" | custom-call | tf_op jit(solution)/shard_map/unmix/pallas_call | solution.py:165
  100.1 0.6 copy-done.18
  100.8 1.0 reshape.34
  101.8 0.7 fusion.x
  102.5 19.3 %reduce.2 = f32[32,8,128]{2,1,0:T(8,128)} custom-call(f32[32,8,128]{2,1,0:T(8,128)} %fusion.x), custom_call_target="tpu_custom_call" | custom-call | tf_op jit(solution)/shard_map/reduce/pallas_call | solution.py:483
  121.8 1.3 %slice.8 = f32[1280]{0:T(1024)} slice(f32[32768]{0:T(1024)} %bitcast.17), slice={[0:1280]} | slice | bytes 10240 | tf_op jit(solution)/shard_map/slice | solution.py:498
  123.1 0.9 slice.9
  124.0 0.6 reshape.37
  124.6 2.7 %copy.15 = bf16[1,640,1280]{2,1,0:T(8,128)(2,1)} copy(bf16[1,640,1280]{2,1,0:T(8,128)(2,1)} %bitcast.16) | data formatting | bytes 3276800
  127.3 1.2 copy.16
  (21 shorter events, 0.1 us)
Async XLA Ops:
  1.3 2.1 %copy-start = (bf16[6,256,1280]{2,1,0:T(8,128)(2,1)S(1)}, bf16[6,256,1280]{2,1,0:T(8,128)(2,1)}, u32[]{:S(2)}) copy-start(bf16[6,256,1280]{2,1,0:T(8,128)(2,1)} %x.5) | copy-start | bytes 11796484
  3.4 2.1 %copy-start.2 = (bf16[6,256,1280]{2,1,0:T(8,128)(2,1)S(1)}, bf16[6,256,1280]{2,1,0:T(8,128)(2,1)}, u32[]{:S(2)}) copy-start(bf16[6,256,1280]{2,1,0:T(8,128)(2,1)} %c.3) | copy-start | bytes 11796484
  5.6 0.8 copy-start.10
  6.3 0.9 copy-start.17
  19.6 1.9 %copy-start.4 = (bf16[6,256,1280]{2,1,0:T(8,128)(2,1)}, bf16[6,256,1280]{2,1,0:T(8,128)(2,1)S(1)}, u32[]{:S(2)}) copy-start(bf16[6,256,1280]{2,1,0:T(8,128)(2,1)S(1)} %get-tuple-element.16.normed) | copy-start | bytes 11796484
  21.5 0.9 copy-start.6
  22.4 0.8 copy-start.9
  23.2 0.6 copy-start.13
  23.8 0.6 copy-start.15
  24.4 54.3 %copy-start.1 = (bf16[6,256,1280]{2,1,0:T(8,128)(2,1)S(1)}, bf16[6,256,1280]{2,1,0:T(8,128)(2,1)}, u32[]{:S(2)}) copy-start(bf16[6,256,1280]{2,1,0:T(8,128)(2,1)} %x.5) | copy-start | bytes 11796484
  24.4 54.3 %copy-start.11 = (bf16[1280,16]{0,1:T(8,128)(2,1)S(1)}, bf16[1280,16]{0,1:T(8,128)(2,1)}, u32[]{:S(2)}) copy-start(bf16[1280,16]{0,1:T(8,128)(2,1)} %param.11) | copy-start | bytes 122884
  24.4 54.3 %copy-start.12 = (bf16[6,32,192]{2,1,0:T(8,128)(2,1)S(1)}, bf16[6,32,192]{2,1,0:T(8,128)(2,1)}, u32[]{:S(2)}) copy-start(bf16[6,32,192]{2,1,0:T(8,128)(2,1)} %constant.8.clone.sel) | copy-start | bytes 221188
  78.7 2.1 %copy-start.3 = (bf16[6,256,1280]{2,1,0:T(8,128)(2,1)S(1)}, bf16[6,256,1280]{2,1,0:T(8,128)(2,1)}, u32[]{:S(2)}) copy-start(bf16[6,256,1280]{2,1,0:T(8,128)(2,1)} %c.3) | copy-start | bytes 11796484
  80.8 2.1 %copy-start.5 = (bf16[6,256,1280]{2,1,0:T(8,128)(2,1)S(1)}, bf16[6,256,1280]{2,1,0:T(8,128)(2,1)}, u32[]{:S(2)}) copy-start(bf16[6,256,1280]{2,1,0:T(8,128)(2,1)} %copy-done.4) | copy-start | bytes 11796484
  83.0 1.1 copy-start.7
  84.1 1.0 copy-start.8
  85.1 0.9 copy-start.14
  86.0 0.9 copy-start.16
  100.1 0.6 copy-start.18
  100.8 26.6 %copy-start.19 = (bf16[1280,640]{1,0:T(8,128)(2,1)S(1)}, bf16[1280,640]{1,0:T(8,128)(2,1)}, u32[]{:S(2)}) copy-start(bf16[1280,640]{1,0:T(8,128)(2,1)} %get-tuple-element.26) | copy-start | bytes 4915204
